TPU v7x, 32 devices: a whole 2x2x4 slice. The times are simulated.
32 devices in a mesh: dp: 16 (over z, y, core), space: 2 (over x).
Axes of the slice: x: 2, y: 2, z: 4, core: 2. Of those that a mesh axis runs over, the one named last changes fastest.
Arguments:
- feature_map: bfloat16 [16, 24, 84, 256], P('dp', 'space'), may hold values from -6 to 6
- proposals: int32 [16, 128, 4], P('dp'), may hold values from 0 to 84, as said below
- hidden_weight: bfloat16 [12544, 512], P(None, 'space'), may hold values from -0.0546875 to 0.0546875
- output_weight: bfloat16 [512, 512], P('space'), may hold values from -0.25 to 0.25
- upstream: bfloat16 [16, 128, 512], P('dp'), may hold values from -6 to 6
Outputs:
- hidden_weight_grad: float32 [12544, 512], P('dp', 'space')
- output_weight_grad: float32 [512, 512], P('space')
- feature_grad: float32 [16, 24, 84, 256], P('dp', 'space')
Inputs may be any that keep to these rules, and one draw needn't show every extreme that they name: `proposals`: each row holds top, left, bottom, right with top < bottom <= 24 and left < right <= 84.
All inputs are finite; a program needn't handle non-finite values.
Results may differ from a plain program's by a relative error of at most 0.012.
Values may be sent and summed in bfloat16 or wider, within the bound.
No kernel may reach another device: no remote copies, remote signals or barrier semaphores. Data moves between devices by JAX's collectives and lax.ppermute only.
A program may use at most 128 MiB of HBM per device.

v0:
```python
import jax
import jax.numpy as jnp
from jax import lax
from jax.sharding import PartitionSpec as P

POOL = 7


def axis_weights(low_edge, high_edge, grid_points):
    edge_start = low_edge.astype(jnp.float32)
    bin_size = (high_edge - low_edge).astype(jnp.float32) / POOL
    bin_index = jnp.arange(POOL).astype(jnp.float32)
    offsets = jnp.array([0.25, 0.75], jnp.float32)
    sample_points = (
        edge_start[:, None, None]
        + (bin_index[None, :, None] + offsets[None, None, :]) * bin_size[:, None, None]
        - 0.5
    )
    weights = jnp.maximum(
        0.0, 1.0 - jnp.abs(sample_points[..., None] - grid_points[None, None, None, :])
    )
    return jnp.mean(weights, axis=2)


def activate(values):
    return jax.nn.gelu(values, approximate=True)


def gelu_grad(values, incoming):
    return jax.vjp(activate, values)[1](incoming)[0]


def block_shape(proposal_count):
    block_size = 32
    return (block_size, proposal_count // block_size)


def crop_rows(own_map, row_weight, col_weight):
    height_cells, width_cells, channels = own_map.shape
    proposal_count = row_weight.shape[0]
    block_size, block_count = block_shape(proposal_count)
    flattened = jnp.transpose(own_map, (1, 0, 2)).reshape(width_cells, height_cells * channels)

    def per_block(blocks):
        row_part, col_part = blocks
        across = jnp.dot(
            col_part.reshape(block_size * POOL, width_cells),
            flattened,
            preferred_element_type=jnp.float32,
        )
        across = across.reshape(block_size, POOL, height_cells, channels)
        return jnp.einsum("riy,rjyc->rijc", row_part, across, precision=lax.Precision.HIGHEST)

    pooled = lax.map(
        per_block,
        (
            row_weight.reshape(block_count, block_size, POOL, height_cells),
            col_weight.reshape(block_count, block_size, POOL, width_cells),
        ),
    )
    return pooled.reshape(proposal_count, POOL * POOL * channels)


def crop_back(grad_pooled, row_weight, col_weight, channels):
    proposal_count, _, height_cells = row_weight.shape
    width_cells = col_weight.shape[2]
    block_size, block_count = block_shape(proposal_count)

    def per_block(running, blocks):
        row_part, col_part, grad_part = blocks
        grad_block = grad_part.reshape(block_size, POOL, POOL, channels)
        spread = jnp.einsum("riy,rijc->rjyc", row_part, grad_block, precision=lax.Precision.HIGHEST)
        added = lax.dot_general(
            col_part.astype(jnp.float32).reshape(block_size * POOL, width_cells),
            spread.reshape(block_size * POOL, height_cells * channels),
            (((0,), (0,)), ((), ())),
            precision=lax.Precision.HIGHEST,
            preferred_element_type=jnp.float32,
        )
        return (running + added, None)

    start = jnp.zeros((width_cells, height_cells * channels), jnp.float32)
    blocks = (
        row_weight.reshape(block_count, block_size, POOL, height_cells),
        col_weight.reshape(block_count, block_size, POOL, width_cells),
        grad_pooled.reshape(block_count, block_size, grad_pooled.shape[1]),
    )
    total, _ = lax.scan(per_block, start, blocks)
    return jnp.transpose(total.reshape(width_cells, height_cells, channels), (1, 0, 2))


def on_device(feature_map, proposals, hidden_weight, output_weight, upstream):
    own_map = feature_map[0]
    corners = proposals[0]
    own_height = own_map.shape[0]
    map_width = own_map.shape[1]
    channels = own_map.shape[2]
    row_offset = lax.axis_index("space") * own_height
    local_grid = (row_offset + jnp.arange(own_height, dtype=jnp.int32)).astype(jnp.float32)
    row_weight = axis_weights(corners[:, 0], corners[:, 2], local_grid)
    col_weight = axis_weights(
        corners[:, 1], corners[:, 3], jnp.arange(map_width, dtype=jnp.int32).astype(jnp.float32)
    ).astype(jnp.bfloat16)
    full_grid = jnp.arange(own_height * lax.axis_size("space"), dtype=jnp.int32).astype(jnp.float32)
    full_weight = axis_weights(corners[:, 0], corners[:, 2], full_grid)
    whole_map = lax.all_gather(own_map, "space", axis=0, tiled=True)
    pooled = crop_rows(whole_map, full_weight, col_weight).astype(jnp.bfloat16)
    pre_hidden = jnp.dot(pooled, hidden_weight, preferred_element_type=jnp.float32)
    hidden = activate(pre_hidden).astype(jnp.bfloat16)
    pre_output = lax.psum(
        jnp.dot(hidden, output_weight, preferred_element_type=jnp.float32).astype(jnp.bfloat16),
        "space",
    ).astype(jnp.float32)
    output_delta = gelu_grad(pre_output, upstream[0].astype(jnp.float32)).astype(jnp.bfloat16)
    step_second = lax.dot_general(
        hidden, output_delta, (((0,), (0,)), ((), ())), preferred_element_type=jnp.float32
    )
    second_total = lax.psum(step_second, "dp")
    hidden_back = lax.dot_general(
        output_delta, output_weight, (((1,), (1,)), ((), ())), preferred_element_type=jnp.float32
    )
    hidden_delta = gelu_grad(pre_hidden, hidden_back).astype(jnp.bfloat16)
    column_rows = lax.all_to_all(pooled, "dp", split_axis=1, concat_axis=0, tiled=True)
    delta_rows = lax.all_gather(hidden_delta, "dp", axis=0, tiled=True)
    first_total = lax.dot_general(
        column_rows, delta_rows, (((0,), (0,)), ((), ())), preferred_element_type=jnp.float32
    )
    partial_grad = lax.dot_general(
        hidden_delta, hidden_weight, (((1,), (1,)), ((), ())), preferred_element_type=jnp.float32
    )
    grad_share = lax.psum_scatter(
        partial_grad.astype(jnp.bfloat16), "space", scatter_dimension=0, tiled=True
    ).astype(jnp.float32)
    pooled_grad = lax.all_gather(
        grad_share.astype(jnp.bfloat16), "space", axis=0, tiled=True
    ).astype(grad_share.dtype)
    map_grad = crop_back(pooled_grad, row_weight, col_weight, channels)
    return (first_total, second_total, map_grad[None])


def solution(mesh):
    placed = (
        P("dp", "space", None, None),
        P("dp", None, None),
        P(None, "space"),
        P("space", None),
        P("dp", None, None),
    )
    return jax.shard_map(
        on_device,
        mesh=mesh,
        in_specs=placed,
        out_specs=(P("dp", "space"), P("space", None), P("dp", "space", None, None)),
        check_vma=False,
    )
```

profile of v0, /device:TPU:0, one launch (start us, length us, event | category | flops | bytes accessed | tf_op | source)
XLA Modules:
  0.0 361.1 jit_solution(6747203176717695255)
XLA Ops:
  11.3 16.2 %all-gather = bf16[1,24,84,256]{3,2,0,1:T(8,128)(2,1)S(1)} all-gather(bf16[1,12,84,256]{3,2,0,1:T(8,128)(2,1)} %bitcast.120), channel_id=2, replica_groups=mesh['dp'=16,'space'=2] {'space'}, dimensions={1}, use_global_device_ids=true | all-gather | bytes 1548288 | tf_op jit(solution)/shard_map/all_gather | solution.py:106
  28.0 34.6 %while.21 = (s32[]{:T(128)}, bf16[4,32,7,7,256]{4,2,3,1,0:T(8,128)(2,1)}, f32[4,32,7,24]{3,2,1,0:T(8,128)S(1)}, bf16[4,32,7,84]{3,1,0,2:T(8,128)(2,1)S(1)}, bf16[84,6144]{1,0:T(8,128)(2,1)S(1)}, /*index=5*/s32[]{:T(128)}) while((s32[]{:T(128)}, bf16[4,32,7,7,256]{4,2,3,1,0:T(8,128)(2,1)}, f32[4,32,7,24]{3,2,1,0:T(8,128)S(1)}, ...), condition=%wide.region_3.4_spmd, body=%wide.region_2.0_spmd.sunk | while | flops 346816512 | bytes 18293832 | solution.py:54
  29.2 7.5 %bitcast_dynamic-update-slice_fusion.2 = bf16[4,32,7,7,256]{4,2,3,1,0:T(8,128)(2,1)} fusion(bf16[4,32,7,7,256]{4,2,3,1,0:T(8,128)(2,1)} %get-tuple-element.230, s32[]{:T(128)} %get-tuple-element.229, f32[32,7,24,256]{3,0,2,1:T(8,128)S(1)} %fusion.66, f32[4,32,7,24]{3,2,1,0:T(8,128)S(1)} %get-tuple-element.237), kind=kOutput, calls=%fused_computation.2.clone.1 | convolution fusion | flops 115605504 | bytes 7472128 | tf_op jit(solution)/shard_map/while/body/eval_jaxpr/riy,rjyc->rijc/dot_general | solution.py:52
  37.8 7.5 %bitcast_dynamic-update-slice_fusion.2 = bf16[4,32,7,7,256]{4,2,3,1,0:T(8,128)(2,1)} fusion(bf16[4,32,7,7,256]{4,2,3,1,0:T(8,128)(2,1)} %get-tuple-element.230, s32[]{:T(128)} %get-tuple-element.229, f32[32,7,24,256]{3,0,2,1:T(8,128)S(1)} %fusion.66, f32[4,32,7,24]{3,2,1,0:T(8,128)S(1)} %get-tuple-element.237), kind=kOutput, calls=%fused_computation.2.clone.1 | convolution fusion | flops 115605504 | bytes 7472128 | tf_op jit(solution)/shard_map/while/body/eval_jaxpr/riy,rjyc->rijc/dot_general | solution.py:52
  46.5 7.5 %bitcast_dynamic-update-slice_fusion.2 = bf16[4,32,7,7,256]{4,2,3,1,0:T(8,128)(2,1)} fusion(bf16[4,32,7,7,256]{4,2,3,1,0:T(8,128)(2,1)} %get-tuple-element.230, s32[]{:T(128)} %get-tuple-element.229, f32[32,7,24,256]{3,0,2,1:T(8,128)S(1)} %fusion.66, f32[4,32,7,24]{3,2,1,0:T(8,128)S(1)} %get-tuple-element.237), kind=kOutput, calls=%fused_computation.2.clone.1 | convolution fusion | flops 115605504 | bytes 7472128 | tf_op jit(solution)/shard_map/while/body/eval_jaxpr/riy,rjyc->rijc/dot_general | solution.py:52
  55.2 7.5 %bitcast_dynamic-update-slice_fusion.2 = bf16[4,32,7,7,256]{4,2,3,1,0:T(8,128)(2,1)} fusion(bf16[4,32,7,7,256]{4,2,3,1,0:T(8,128)(2,1)} %get-tuple-element.230, s32[]{:T(128)} %get-tuple-element.229, f32[32,7,24,256]{3,0,2,1:T(8,128)S(1)} %fusion.66, f32[4,32,7,24]{3,2,1,0:T(8,128)S(1)} %get-tuple-element.237), kind=kOutput, calls=%fused_computation.2.clone.1 | convolution fusion | flops 115605504 | bytes 7472128 | tf_op jit(solution)/shard_map/while/body/eval_jaxpr/riy,rjyc->rijc/dot_general | solution.py:52
  62.6 5.1 %copy.77 = bf16[4,32,7,7,256]{4,3,2,1,0:T(8,128)(2,1)} copy(bf16[4,32,7,7,256]{4,2,3,1,0:T(8,128)(2,1)} %get-tuple-element.57) | data formatting | bytes 6422528 | tf_op jit(solution)/shard_map/convert_element_type | solution.py:107
  67.8 5.6 %convert_element_type.132 = bf16[128,12544]{1,0:T(8,128)(2,1)S(1)} reshape(bf16[4,32,7,7,256]{4,3,2,1,0:T(8,128)(2,1)} %copy.77) | data formatting | bytes 6422528 | tf_op jit(solution)/shard_map/convert_element_type | solution.py:107
  73.4 3.8 %fusion.39 = f32[128,256]{1,0:T(8,128)S(1)} fusion(bf16[128,12544]{1,0:T(8,128)(2,1)S(1)} %convert_element_type.132, bf16[12544,256]{1,0:T(8,128)(2,1)} %param.14), kind=kOutput, calls=%fused_computation.69 | convolution fusion | flops 822083584 | bytes 9764864 | tf_op jit(solution)/shard_map/dot_general | solution.py:108
  79.0 22.9 %all-reduce.3.cloned.1.call-done = bf16[128,512]{1,0:T(8,128)(2,1)} async-done(((bf16[128,512]{1,0:T(8,128)(2,1)}), bf16[128,512]{1,0:T(8,128)(2,1)}) %all-reduce.3.cloned.1.call-update) | async-done | bytes 131088 | tf_op jit(solution)/shard_map/psum | solution.py:110
  104.9 6.8 %convolution_convert_fusion = bf16[128,12544]{1,0:T(8,128)(2,1)} fusion(bf16[128,256]{1,0:T(8,128)(2,1)S(1)} %fusion.37, bf16[12544,256]{1,0:T(8,128)(2,1)} %param.14), kind=kOutput, calls=%fused_computation.21 | convolution fusion | flops 823689216 | bytes 9699328 | tf_op jit(solution)/shard_map/dot_general | solution.py:128
  111.7 9.3 %convert_element_type.129 = bf16[128,16,784]{2,1,0:T(8,128)(2,1)} reshape(bf16[4,32,7,7,256]{4,3,2,1,0:T(8,128)(2,1)} %copy.77) | data formatting | bytes 6422528 | tf_op jit(solution)/shard_map/convert_element_type | solution.py:107
  121.0 6.2 %copy.78 = bf16[128,16,784]{0,2,1:T(8,128)(2,1)} copy(bf16[128,16,784]{2,1,0:T(8,128)(2,1)} %convert_element_type.129) | data formatting | bytes 6422528 | tf_op jit(solution)/shard_map/convert_element_type | solution.py:107
  127.2 5.8 %all-to-all-start = ((bf16[128,16,784]{0,2,1:T(8,128)(2,1)}), bf16[128,16,784]{0,2,1:T(8,128)(2,1)S(1)}, u32[]{:S(2)}, u32[]{:S(2)}) async-start(bf16[128,16,784]{0,2,1:T(8,128)(2,1)} %copy.78), calls=%async_computation | async-start | bytes 6422528 | tf_op jit(solution)/shard_map/all_to_all | solution.py:123
  133.8 22.2 %reduce-scatter.2.cloned.1.call-done = bf16[64,12544]{1,0:T(8,128)(2,1)} async-done(((bf16[128,12544]{1,0:T(8,128)(2,1)}), bf16[64,12544]{1,0:T(8,128)(2,1)}) %reduce-scatter.2.cloned.1.call-update) | async-done | bytes 1605648 | tf_op jit(solution)/shard_map/reduce_scatter | solution.py:131
  160.2 50.5 %all-gather.4.cloned.1.call-done = bf16[2048,256]{1,0:T(8,128)(2,1)} async-done(((bf16[128,256]{1,0:T(8,128)(2,1)}), bf16[2048,256]{1,0:T(8,128)(2,1)}) %all-gather.4.cloned.1.call-update) | async-done | bytes 1048592 | tf_op jit(solution)/shard_map/all_gather | solution.py:124
  213.9 44.3 %all-gather.6.cloned.1.call-done = bf16[128,12544]{1,0:T(8,128)(2,1)} async-done(((bf16[64,12544]{1,0:T(8,128)(2,1)}), bf16[128,12544]{1,0:T(8,128)(2,1)}) %all-gather.6.cloned.1.call-update) | async-done | bytes 3211280 | tf_op jit(solution)/shard_map/all_gather | solution.py:134
  258.2 5.1 %convert.3 = f32[4,32,12544]{2,1,0:T(8,128)} convert(bf16[4,32,12544]{2,1,0:T(8,128)(2,1)} %bitcast.115) | non-fusion elementwise | flops 1605632 | bytes 9633792 | tf_op jit(solution)/shard_map/reshape | solution.py:86
  263.3 51.9 %while.22 = (s32[]{:T(128)}, f32[84,3072]{1,0:T(8,128)}, bf16[4,32,7,84]{3,2,1,0:T(8,128)(2,1)}, f32[4,32,12544]{2,1,0:T(8,128)}, f32[4,32,7,12]{3,2,1,0:T(8,128)}, /*index=5*/s32[]{:T(128)}, s32[]{:T(128)}) while((s32[]{:T(128)}, f32[84,3072]{1,0:T(8,128)}, bf16[4,32,7,84]{3,2,1,0:T(8,128)(2,1)}, f32[4,32,12544]{2,1,0:T(8,128)}, ...), condition=%wide.region_9.10_spmd.clone, body=%wide.region_8.9_spmd.clone.sunk | while | flops 751951872 | bytes 21422432 | solution.py:88
  265.3 4.5 %fusion.71 = f32[32,7,256,12]{2,3,1,0:T(8,128)S(1)} fusion(f32[32,7,7,256]{3,2,1,0:T(8,128)S(1)} %reshape.239, f32[4,32,7,12]{3,2,1,0:T(8,128)} %get-tuple-element.259, s32[]{:T(128)} %get-tuple-element.248), kind=kOutput, calls=%fused_computation.14.clone.1 | convolution fusion | flops 57802752 | bytes 4489728 | tf_op jit(solution)/shard_map/while/body/eval_jaxpr/riy,rijc->rjyc/dot_general | solution.py:72
  277.3 4.5 %fusion.71 = f32[32,7,256,12]{2,3,1,0:T(8,128)S(1)} fusion(f32[32,7,7,256]{3,2,1,0:T(8,128)S(1)} %reshape.239, f32[4,32,7,12]{3,2,1,0:T(8,128)} %get-tuple-element.259, s32[]{:T(128)} %get-tuple-element.248), kind=kOutput, calls=%fused_computation.14.clone.1 | convolution fusion | flops 57802752 | bytes 4489728 | tf_op jit(solution)/shard_map/while/body/eval_jaxpr/riy,rijc->rjyc/dot_general | solution.py:72
  290.6 4.5 %fusion.71 = f32[32,7,256,12]{2,3,1,0:T(8,128)S(1)} fusion(f32[32,7,7,256]{3,2,1,0:T(8,128)S(1)} %reshape.239, f32[4,32,7,12]{3,2,1,0:T(8,128)} %get-tuple-element.259, s32[]{:T(128)} %get-tuple-element.248), kind=kOutput, calls=%fused_computation.14.clone.1 | convolution fusion | flops 57802752 | bytes 4489728 | tf_op jit(solution)/shard_map/while/body/eval_jaxpr/riy,rijc->rjyc/dot_general | solution.py:72
  303.9 4.5 %fusion.71 = f32[32,7,256,12]{2,3,1,0:T(8,128)S(1)} fusion(f32[32,7,7,256]{3,2,1,0:T(8,128)S(1)} %reshape.239, f32[4,32,7,12]{3,2,1,0:T(8,128)} %get-tuple-element.259, s32[]{:T(128)} %get-tuple-element.248), kind=kOutput, calls=%fused_computation.14.clone.1 | convolution fusion | flops 57802752 | bytes 4489728 | tf_op jit(solution)/shard_map/while/body/eval_jaxpr/riy,rijc->rjyc/dot_general | solution.py:72
  318.8 33.9 %all-reduce.5.cloned.1.call-done = f32[256,512]{1,0:T(8,128)} async-done(((f32[256,512]{1,0:T(8,128)}), f32[256,512]{1,0:T(8,128)}) %all-reduce.5.cloned.1.call-update) | async-done | bytes 524304 | tf_op jit(solution)/shard_map/psum | solution.py:118
  (94 shorter events, 61.4 us)
Async XLA Ops:
  7.2 70.7 %copy-start = (bf16[256,512]{1,0:T(8,128)(2,1)S(1)}, bf16[256,512]{1,0:T(8,128)(2,1)}, u32[]{:S(2)}) copy-start(bf16[256,512]{1,0:T(8,128)(2,1)} %param.15) | copy-start | bytes 786436
  7.2 94.7 %all-reduce.3.cloned.1.call-start = ((), (), s32[]{:S(2)}) async-start(), calls=%async_computation.2 | async-start | bytes 262144 | tf_op jit(solution)/shard_map/psum | solution.py:110
  10.7 17.0 %copy-start.2 = (bf16[128,7,84]{0,2,1:T(8,128)(2,1)}, bf16[128,7,84]{0,2,1:T(8,128)(2,1)S(1)}, u32[]{:S(2)}) copy-start(bf16[128,7,84]{0,2,1:T(8,128)(2,1)S(1)} %multiply_convert_fusion) | copy-start | bytes 451588
  77.2 0.7 copy-start.4
  78.7 77.3 %reduce-scatter.2.cloned.1.call-start = ((), (), s32[]{:S(2)}) async-start(), calls=%async_computation.5 | async-start | bytes 4816896 | tf_op jit(solution)/shard_map/reduce_scatter | solution.py:131
  103.0 0.6 copy-start.6
  104.8 6.8 %copy-start.7 = (bf16[128,256]{1,0:T(8,128)(2,1)}, bf16[128,256]{1,0:T(8,128)(2,1)S(1)}, u32[]{:S(2)}) copy-start(bf16[128,256]{1,0:T(8,128)(2,1)S(1)} %fusion.37) | copy-start | bytes 196612
  127.2 28.8 %copy-start.3 = (bf16[128,7,84]{0,2,1:T(8,128)(2,1)S(1)}, bf16[128,7,84]{0,2,1:T(8,128)(2,1)}, u32[]{:S(2)}) copy-start(bf16[128,7,84]{0,2,1:T(8,128)(2,1)} %copy-done.2) | copy-start | bytes 451588
  127.2 31.0 %copy-start.5 = (f32[128,256]{1,0:T(8,128)S(1)}, f32[128,256]{1,0:T(8,128)}, u32[]{:S(2)}) copy-start(f32[128,256]{1,0:T(8,128)} %copy-done.4) | copy-start | bytes 393220
  127.2 83.6 %all-to-all-start = ((bf16[128,16,784]{0,2,1:T(8,128)(2,1)}), bf16[128,16,784]{0,2,1:T(8,128)(2,1)S(1)}, u32[]{:S(2)}, u32[]{:S(2)}) async-start(bf16[128,16,784]{0,2,1:T(8,128)(2,1)} %copy.78), calls=%async_computation | async-start | bytes 6422528 | tf_op jit(solution)/shard_map/all_to_all | solution.py:123
  133.0 77.8 %all-gather.4.cloned.1.call-start = ((), (), s32[]{:S(2)}) async-start(), calls=%async_computation.3 | async-start | bytes 1114112 | tf_op jit(solution)/shard_map/all_gather | solution.py:124
  133.7 124.4 %all-gather.6.cloned.1.call-start = ((), (), s32[]{:S(2)}) async-start(), calls=%async_computation.6 | async-start | bytes 4816896 | tf_op jit(solution)/shard_map/all_gather | solution.py:134
  156.0 196.7 %all-reduce.5.cloned.1.call-start = ((), (), s32[]{:S(2)}) async-start(), calls=%async_computation.4 | async-start | bytes 1048576 | tf_op jit(solution)/shard_map/psum | solution.py:118
  315.2 39.4 %copy-start.1 = (bf16[256,512]{1,0:T(8,128)(2,1)S(1)}, bf16[256,512]{1,0:T(8,128)(2,1)}, u32[]{:S(2)}) copy-start(bf16[256,512]{1,0:T(8,128)(2,1)} %param.15) | copy-start | bytes 786436
Sparse Core Ops, SparseCore 0:
  78.9 22.9 all-reduce.2
  111.8 44.1 reduce-scatter.1
  158.2 52.5 all-gather.3
  212.2 45.9 all-gather.5
  262.0 90.6 all-reduce.4
where the time goes:
time: 363 us; the launch traced here: 361 us
  waiting for transfers between devices  175 us (48%)
  matrix products  81.6 us (22%)
  local copies, waits for them, and re-layouts  58.4 us (16%)
  blocking collectives  16.2 us (4%)
  between operations  14 us (4%)
  other arithmetic  10.1 us (3%)
  starting transfers between devices  6.13 us (2%)
    all_gather x1, waiting for transfers between devices, on_device(): delta_rows = lax.all_gather(hidden_delta, 'dp', axis=0, tiled=True)  50.5 us
    all_gather x1, waiting for transfers between devices, on_device(): lax.all_gather(grad_share.astype(jnp.bfloat16), 'space', axis=0, tiled=True)  44.3 us
    psum x1, waiting for transfers between devices, on_device(): second_total = lax.psum(step_second, 'dp')  33.9 us
    dot_general x4, matrix products, per_block(): jnp.einsum('riy,rjyc->rijc', row_part, across, precision=lax.Precision.HI...  29.9 us
    convert_element_type x4, local copies, waits for them, and re-layouts, on_device(): pooled = crop_rows(whole_map, full_weight, col_weight).astype(jnp.bfloat16)  26.3 us
    psum x1, waiting for transfers between devices, on_device(): lax.psum(jnp.dot(hidden, output_weight, preferred_element_type=jnp.float3...  22.9 us
    reduce_scatter x1, waiting for transfers between devices, on_device(): lax.psum_scatter(partial_grad.astype(jnp.bfloat16), 'space', scatter_dime...  22.2 us
    dot_general x4, matrix products, per_block(): jnp.einsum('riy,rijc->rjyc', row_part, grad_block, precision=lax.Precisio...  17.9 us
  transfers between devices with their start and end apart: 6, of which 5 were waited for; matrix products, arithmetic and copies ran while one was open for 23% of the time, Pallas kernels for 0%

commit v1 on v0

--- a/solution.py
+++ b/solution.py
@@ -4,6 +4,14 @@
 from jax.sharding import PartitionSpec as P
 
 POOL = 7
+
+
+def add_in_pairs(array, axis):
+    n_dev, acc = (lax.axis_size(axis), array)
+    for far in [1 << k for k in range(n_dev.bit_length() - 1)]:
+        swap = [(i, i ^ far) for i in range(n_dev)]
+        acc = acc + lax.ppermute(acc, axis, swap)
+    return acc
 
 
 def axis_weights(low_edge, high_edge, grid_points):
@@ -115,7 +123,7 @@
     step_second = lax.dot_general(
         hidden, output_delta, (((0,), (0,)), ((), ())), preferred_element_type=jnp.float32
     )
-    second_total = lax.psum(step_second, "dp")
+    second_total = add_in_pairs(step_second, "dp")
     hidden_back = lax.dot_general(
         output_delta, output_weight, (((1,), (1,)), ((), ())), preferred_element_type=jnp.float32
     )

time: 363 us -> 330 us (0.909)
  waiting for transfers between devices: 175 us -> 133 us
  starting transfers between devices: 6.13 us -> 15 us
    ppermute x0 -> x4, waiting for transfers between devices: none -> 69.7 us  [add_in_pairs(): acc = acc + lax.ppermute(acc, axis, swap)]
    all_gather x1, waiting for transfers between devices: 50.5 us -> 0.01 us  [on_device(): delta_rows = lax.all_gather(hidden_delta, 'dp', axis=0, tiled=True)]
    psum x1 -> x0, waiting for transfers between devices: 33.9 us -> none  [on_device(): second_total = lax.psum(step_second, 'dp')]
    all_gather x1, waiting for transfers between devices: 44.3 us -> 17 us  [on_device(): lax.all_gather(grad_share.astype(jnp.bfloat16), 'space', axis=0, tiled=True)]
    ppermute x0 -> x4, starting transfers between devices: none -> 8.9 us  [add_in_pairs(): acc = acc + lax.ppermute(acc, axis, swap)]
  transfers between devices with their start and end apart: 6 -> 9, of which waited for: 5 -> 7; matrix products, arithmetic and copies ran while one was open for 23% -> 8% of each run, Pallas kernels for 0% -> 0%
where the time goes in v1:
time: 330 us; the launch traced here: 329 us
  waiting for transfers between devices  133 us (40%)
  matrix products  80.9 us (25%)
  local copies, waits for them, and re-layouts  56.5 us (17%)
  blocking collectives  16.2 us (5%)
  starting transfers between devices  15 us (5%)
  between operations  14 us (4%)
  other arithmetic  13.2 us (4%)
    ppermute x4, waiting for transfers between devices, add_in_pairs(): acc = acc + lax.ppermute(acc, axis, swap)  69.7 us
    dot_general x4, matrix products, per_block(): jnp.einsum('riy,rjyc->rijc', row_part, across, precision=lax.Precision.HI...  29.9 us
    convert_element_type x4, local copies, waits for them, and re-layouts, on_device(): pooled = crop_rows(whole_map, full_weight, col_weight).astype(jnp.bfloat16)  26.3 us
    psum x1, waiting for transfers between devices, on_device(): lax.psum(jnp.dot(hidden, output_weight, preferred_element_type=jnp.float3...  22.9 us
    reduce_scatter x1, waiting for transfers between devices, on_device(): lax.psum_scatter(partial_grad.astype(jnp.bfloat16), 'space', scatter_dime...  22.2 us
    dot_general x4, matrix products, per_block(): jnp.einsum('riy,rijc->rjyc', row_part, grad_block, precision=lax.Precisio...  17.9 us
    all_gather x1, waiting for transfers between devices, on_device(): lax.all_gather(grad_share.astype(jnp.bfloat16), 'space', axis=0, tiled=True)  17 us
    all_gather x1, blocking collectives, on_device(): whole_map = lax.all_gather(own_map, 'space', axis=0, tiled=True)  16.2 us
  transfers between devices with their start and end apart: 9, of which 7 were waited for; matrix products, arithmetic and copies ran while one was open for 8% of the time, Pallas kernels for 0%

profile of v1, /device:TPU:0, one launch (start us, length us, event | category | flops | bytes accessed | tf_op | source)
XLA Modules:
  0.0 328.5 jit_solution(246690148872526134)
XLA Ops:
  11.3 16.2 %all-gather = bf16[1,24,84,256]{3,2,0,1:T(8,128)(2,1)S(1)} all-gather(bf16[1,12,84,256]{3,2,0,1:T(8,128)(2,1)} %bitcast.120), channel_id=2, replica_groups=mesh['dp'=16,'space'=2] {'space'}, dimensions={1}, use_global_device_ids=true | all-gather | bytes 1548288 | tf_op jit(solution)/shard_map/all_gather | solution.py:114
  28.0 34.6 %while.21 = (s32[]{:T(128)}, bf16[4,32,7,7,256]{4,2,3,1,0:T(8,128)(2,1)}, f32[4,32,7,24]{3,2,1,0:T(8,128)S(1)}, bf16[4,32,7,84]{3,1,0,2:T(8,128)(2,1)S(1)}, bf16[84,6144]{1,0:T(8,128)(2,1)S(1)}, /*index=5*/s32[]{:T(128)}) while((s32[]{:T(128)}, bf16[4,32,7,7,256]{4,2,3,1,0:T(8,128)(2,1)}, f32[4,32,7,24]{3,2,1,0:T(8,128)S(1)}, ...), condition=%wide.region_3.4_spmd, body=%wide.region_2.0_spmd.sunk | while | flops 346816512 | bytes 18293832 | solution.py:62
  29.2 7.5 %bitcast_dynamic-update-slice_fusion.2 = bf16[4,32,7,7,256]{4,2,3,1,0:T(8,128)(2,1)} fusion(bf16[4,32,7,7,256]{4,2,3,1,0:T(8,128)(2,1)} %get-tuple-element.230, s32[]{:T(128)} %get-tuple-element.229, f32[32,7,24,256]{3,0,2,1:T(8,128)S(1)} %fusion.66, f32[4,32,7,24]{3,2,1,0:T(8,128)S(1)} %get-tuple-element.237), kind=kOutput, calls=%fused_computation.2.clone.1 | convolution fusion | flops 115605504 | bytes 7472128 | tf_op jit(solution)/shard_map/while/body/eval_jaxpr/riy,rjyc->rijc/dot_general | solution.py:60
  37.9 7.5 %bitcast_dynamic-update-slice_fusion.2 = bf16[4,32,7,7,256]{4,2,3,1,0:T(8,128)(2,1)} fusion(bf16[4,32,7,7,256]{4,2,3,1,0:T(8,128)(2,1)} %get-tuple-element.230, s32[]{:T(128)} %get-tuple-element.229, f32[32,7,24,256]{3,0,2,1:T(8,128)S(1)} %fusion.66, f32[4,32,7,24]{3,2,1,0:T(8,128)S(1)} %get-tuple-element.237), kind=kOutput, calls=%fused_computation.2.clone.1 | convolution fusion | flops 115605504 | bytes 7472128 | tf_op jit(solution)/shard_map/while/body/eval_jaxpr/riy,rjyc->rijc/dot_general | solution.py:60
  46.5 7.5 %bitcast_dynamic-update-slice_fusion.2 = bf16[4,32,7,7,256]{4,2,3,1,0:T(8,128)(2,1)} fusion(bf16[4,32,7,7,256]{4,2,3,1,0:T(8,128)(2,1)} %get-tuple-element.230, s32[]{:T(128)} %get-tuple-element.229, f32[32,7,24,256]{3,0,2,1:T(8,128)S(1)} %fusion.66, f32[4,32,7,24]{3,2,1,0:T(8,128)S(1)} %get-tuple-element.237), kind=kOutput, calls=%fused_computation.2.clone.1 | convolution fusion | flops 115605504 | bytes 7472128 | tf_op jit(solution)/shard_map/while/body/eval_jaxpr/riy,rjyc->rijc/dot_general | solution.py:60
  55.2 7.5 %bitcast_dynamic-update-slice_fusion.2 = bf16[4,32,7,7,256]{4,2,3,1,0:T(8,128)(2,1)} fusion(bf16[4,32,7,7,256]{4,2,3,1,0:T(8,128)(2,1)} %get-tuple-element.230, s32[]{:T(128)} %get-tuple-element.229, f32[32,7,24,256]{3,0,2,1:T(8,128)S(1)} %fusion.66, f32[4,32,7,24]{3,2,1,0:T(8,128)S(1)} %get-tuple-element.237), kind=kOutput, calls=%fused_computation.2.clone.1 | convolution fusion | flops 115605504 | bytes 7472128 | tf_op jit(solution)/shard_map/while/body/eval_jaxpr/riy,rjyc->rijc/dot_general | solution.py:60
  62.6 5.1 %copy.77 = bf16[4,32,7,7,256]{4,3,2,1,0:T(8,128)(2,1)} copy(bf16[4,32,7,7,256]{4,2,3,1,0:T(8,128)(2,1)} %get-tuple-element.57) | data formatting | bytes 6422528 | tf_op jit(solution)/shard_map/convert_element_type | solution.py:115
  67.8 5.6 %convert_element_type.132 = bf16[128,12544]{1,0:T(8,128)(2,1)S(1)} reshape(bf16[4,32,7,7,256]{4,3,2,1,0:T(8,128)(2,1)} %copy.77) | data formatting | bytes 6422528 | tf_op jit(solution)/shard_map/convert_element_type | solution.py:115
  79.0 22.9 %all-reduce.2.cloned.1.call-done = bf16[128,512]{1,0:T(8,128)(2,1)} async-done(((bf16[128,512]{1,0:T(8,128)(2,1)}), bf16[128,512]{1,0:T(8,128)(2,1)}) %all-reduce.2.cloned.1.call-update) | async-done | bytes 131088 | tf_op jit(solution)/shard_map/psum | solution.py:118
  104.9 6.8 %convolution_convert_fusion = bf16[128,12544]{1,0:T(8,128)(2,1)} fusion(bf16[128,256]{1,0:T(8,128)(2,1)S(1)} %fusion.37, bf16[12544,256]{1,0:T(8,128)(2,1)} %param.14), kind=kOutput, calls=%fused_computation.21 | convolution fusion | flops 823689216 | bytes 9699328 | tf_op jit(solution)/shard_map/dot_general | solution.py:136
  111.7 9.3 %convert_element_type.129 = bf16[128,16,784]{2,1,0:T(8,128)(2,1)} reshape(bf16[4,32,7,7,256]{4,3,2,1,0:T(8,128)(2,1)} %copy.77) | data formatting | bytes 6422528 | tf_op jit(solution)/shard_map/convert_element_type | solution.py:115
  121.0 6.2 %copy.78 = bf16[128,16,784]{0,2,1:T(8,128)(2,1)} copy(bf16[128,16,784]{2,1,0:T(8,128)(2,1)} %convert_element_type.129) | data formatting | bytes 6422528 | tf_op jit(solution)/shard_map/convert_element_type | solution.py:115
  127.3 5.8 %all-to-all-start = ((bf16[128,16,784]{0,2,1:T(8,128)(2,1)}), bf16[128,16,784]{0,2,1:T(8,128)(2,1)S(1)}, u32[]{:S(2)}, u32[]{:S(2)}) async-start(bf16[128,16,784]{0,2,1:T(8,128)(2,1)} %copy.78), calls=%async_computation | async-start | bytes 6422528 | tf_op jit(solution)/shard_map/all_to_all | solution.py:131
  133.8 22.2 %reduce-scatter.2.cloned.1.call-done = bf16[64,12544]{1,0:T(8,128)(2,1)} async-done(((bf16[128,12544]{1,0:T(8,128)(2,1)}), bf16[64,12544]{1,0:T(8,128)(2,1)}) %reduce-scatter.2.cloned.1.call-update) | async-done | bytes 1605648 | tf_op jit(solution)/shard_map/reduce_scatter | solution.py:139
  160.9 21.7 %collective-permute-done.1 = f32[256,512]{1,0:T(8,128)S(1)} collective-permute-done((f32[256,512]{1,0:T(8,128)S(1)}, f32[256,512]{1,0:T(8,128)S(1)}, u32[]{:S(2)}, u32[]{:S(2)}) %collective-permute-start.1) | collective-permute-done | bytes 524320 | tf_op jit(solution)/shard_map/ppermute | solution.py:13
  184.1 24.8 %collective-permute-done.2 = f32[256,512]{1,0:T(8,128)S(1)} collective-permute-done((f32[256,512]{1,0:T(8,128)S(1)}, f32[256,512]{1,0:T(8,128)S(1)}, u32[]{:S(2)}, u32[]{:S(2)}) %collective-permute-start.2) | collective-permute-done | bytes 524320 | tf_op jit(solution)/shard_map/ppermute | solution.py:13
  209.7 5.8 %collective-permute-start.3 = (f32[256,512]{1,0:T(8,128)}, f32[256,512]{1,0:T(8,128)}, u32[]{:S(2)}, u32[]{:S(2)}) collective-permute-start(f32[256,512]{1,0:T(8,128)} %add.169), channel_id=1, source_target_pairs={{0,16},{2,18},{4,20},{6,22},{8,24},{10,26},{12,28},{14,30},{16,0},... | collective-permute-start | bytes 1572872 | tf_op jit(solution)/shard_map/ppermute | solution.py:13
  217.8 21.4 %collective-permute-done.3 = f32[256,512]{1,0:T(8,128)} collective-permute-done((f32[256,512]{1,0:T(8,128)}, f32[256,512]{1,0:T(8,128)}, u32[]{:S(2)}, u32[]{:S(2)}) %collective-permute-start.3) | collective-permute-done | bytes 524320 | tf_op jit(solution)/shard_map/ppermute | solution.py:13
  244.3 17.0 %all-gather.6.cloned.1.call-done = bf16[128,12544]{1,0:T(8,128)(2,1)} async-done(((bf16[64,12544]{1,0:T(8,128)(2,1)}), bf16[128,12544]{1,0:T(8,128)(2,1)}) %all-gather.6.cloned.1.call-update) | async-done | bytes 3211280 | tf_op jit(solution)/shard_map/all_gather | solution.py:142
  261.3 5.1 %convert.3 = f32[4,32,12544]{2,1,0:T(8,128)} convert(bf16[4,32,12544]{2,1,0:T(8,128)(2,1)} %bitcast.115) | non-fusion elementwise | flops 1605632 | bytes 9633792 | tf_op jit(solution)/shard_map/reshape | solution.py:94
  266.5 51.9 %while.22 = (s32[]{:T(128)}, f32[84,3072]{1,0:T(8,128)}, bf16[4,32,7,84]{3,2,1,0:T(8,128)(2,1)}, f32[4,32,12544]{2,1,0:T(8,128)}, f32[4,32,7,12]{3,2,1,0:T(8,128)}, /*index=5*/s32[]{:T(128)}, s32[]{:T(128)}) while((s32[]{:T(128)}, f32[84,3072]{1,0:T(8,128)}, bf16[4,32,7,84]{3,2,1,0:T(8,128)(2,1)}, f32[4,32,12544]{2,1,0:T(8,128)}, ...), condition=%wide.region_8.9_spmd.clone, body=%wide.region_7.8_spmd.clone.sunk | while | flops 751951872 | bytes 21422432 | solution.py:96
  268.4 4.5 %fusion.71 = f32[32,7,256,12]{2,3,1,0:T(8,128)S(1)} fusion(f32[32,7,7,256]{3,2,1,0:T(8,128)S(1)} %reshape.239, f32[4,32,7,12]{3,2,1,0:T(8,128)} %get-tuple-element.259, s32[]{:T(128)} %get-tuple-element.248), kind=kOutput, calls=%fused_computation.14.clone.1 | convolution fusion | flops 57802752 | bytes 4489728 | tf_op jit(solution)/shard_map/while/body/eval_jaxpr/riy,rijc->rjyc/dot_general | solution.py:80
  280.5 4.5 %fusion.71 = f32[32,7,256,12]{2,3,1,0:T(8,128)S(1)} fusion(f32[32,7,7,256]{3,2,1,0:T(8,128)S(1)} %reshape.239, f32[4,32,7,12]{3,2,1,0:T(8,128)} %get-tuple-element.259, s32[]{:T(128)} %get-tuple-element.248), kind=kOutput, calls=%fused_computation.14.clone.1 | convolution fusion | flops 57802752 | bytes 4489728 | tf_op jit(solution)/shard_map/while/body/eval_jaxpr/riy,rijc->rjyc/dot_general | solution.py:80
  307.1 4.5 %fusion.71 = f32[32,7,256,12]{2,3,1,0:T(8,128)S(1)} fusion(f32[32,7,7,256]{3,2,1,0:T(8,128)S(1)} %reshape.239, f32[4,32,7,12]{3,2,1,0:T(8,128)} %get-tuple-element.259, s32[]{:T(128)} %get-tuple-element.248), kind=kOutput, calls=%fused_computation.14.clone.1 | convolution fusion | flops 57802752 | bytes 4489728 | tf_op jit(solution)/shard_map/while/body/eval_jaxpr/riy,rijc->rjyc/dot_general | solution.py:80
  (102 shorter events, 75.1 us)
Async XLA Ops:
  7.2 70.7 %copy-start = (bf16[256,512]{1,0:T(8,128)(2,1)S(1)}, bf16[256,512]{1,0:T(8,128)(2,1)}, u32[]{:S(2)}) copy-start(bf16[256,512]{1,0:T(8,128)(2,1)} %param.15) | copy-start | bytes 786436
  7.2 94.7 %all-reduce.2.cloned.1.call-start = ((), (), s32[]{:S(2)}) async-start(), calls=%async_computation.2 | async-start | bytes 262144 | tf_op jit(solution)/shard_map/psum | solution.py:118
  10.7 17.0 %copy-start.2 = (bf16[128,7,84]{0,2,1:T(8,128)(2,1)}, bf16[128,7,84]{0,2,1:T(8,128)(2,1)S(1)}, u32[]{:S(2)}) copy-start(bf16[128,7,84]{0,2,1:T(8,128)(2,1)S(1)} %multiply_convert_fusion) | copy-start | bytes 451588
  77.2 0.7 copy-start.4
  78.8 77.3 %reduce-scatter.2.cloned.1.call-start = ((), (), s32[]{:S(2)}) async-start(), calls=%async_computation.4 | async-start | bytes 4816896 | tf_op jit(solution)/shard_map/reduce_scatter | solution.py:139
  103.1 0.7 copy-start.6
  104.9 6.8 %copy-start.7 = (bf16[128,256]{1,0:T(8,128)(2,1)}, bf16[128,256]{1,0:T(8,128)(2,1)S(1)}, u32[]{:S(2)}) copy-start(bf16[128,256]{1,0:T(8,128)(2,1)S(1)} %fusion.37) | copy-start | bytes 196612
  127.3 28.8 %copy-start.5 = (f32[128,256]{1,0:T(8,128)S(1)}, f32[128,256]{1,0:T(8,128)}, u32[]{:S(2)}) copy-start(f32[128,256]{1,0:T(8,128)} %copy-done.4) | copy-start | bytes 393220
  127.3 114.0 %all-to-all-start = ((bf16[128,16,784]{0,2,1:T(8,128)(2,1)}), bf16[128,16,784]{0,2,1:T(8,128)(2,1)S(1)}, u32[]{:S(2)}, u32[]{:S(2)}) async-start(bf16[128,16,784]{0,2,1:T(8,128)(2,1)} %copy.78), calls=%async_computation | async-start | bytes 6422528 | tf_op jit(solution)/shard_map/all_to_all | solution.py:131
  133.0 108.2 %all-gather.4.cloned.1.call-start = ((), (), s32[]{:S(2)}) async-start(), calls=%async_computation.3 | async-start | bytes 1114112 | tf_op jit(solution)/shard_map/all_gather | solution.py:132
  133.8 127.6 %all-gather.6.cloned.1.call-start = ((), (), s32[]{:S(2)}) async-start(), calls=%async_computation.5 | async-start | bytes 4816896 | tf_op jit(solution)/shard_map/all_gather | solution.py:142
  156.0 59.5 %copy-start.3 = (bf16[128,7,84]{0,2,1:T(8,128)(2,1)S(1)}, bf16[128,7,84]{0,2,1:T(8,128)(2,1)}, u32[]{:S(2)}) copy-start(bf16[128,7,84]{0,2,1:T(8,128)(2,1)} %copy-done.2) | copy-start | bytes 451588
  157.3 2.0 collective-permute-start
  159.3 23.2 %collective-permute-start.1 = (f32[256,512]{1,0:T(8,128)S(1)}, f32[256,512]{1,0:T(8,128)S(1)}, u32[]{:S(2)}, u32[]{:S(2)}) collective-permute-start(f32[256,512]{1,0:T(8,128)S(1)} %add.167), channel_id=1, source_target_pairs={{0,4},{2,6},{4,0},{6,2},{8,12},{10,14},{12,8},{14,10},{16,20},{18,... | collective-permute-start | bytes 1572872 | tf_op jit(solution)/shard_map/ppermute | solution.py:13
  182.6 26.2 %collective-permute-start.2 = (f32[256,512]{1,0:T(8,128)S(1)}, f32[256,512]{1,0:T(8,128)S(1)}, u32[]{:S(2)}, u32[]{:S(2)}) collective-permute-start(f32[256,512]{1,0:T(8,128)S(1)} %add.168), channel_id=1, source_target_pairs={{0,8},{2,10},{4,12},{6,14},{8,0},{10,2},{12,4},{14,6},{16,24},{18,... | collective-permute-start | bytes 1572872 | tf_op jit(solution)/shard_map/ppermute | solution.py:13
  209.7 29.4 %collective-permute-start.3 = (f32[256,512]{1,0:T(8,128)}, f32[256,512]{1,0:T(8,128)}, u32[]{:S(2)}, u32[]{:S(2)}) collective-permute-start(f32[256,512]{1,0:T(8,128)} %add.169), channel_id=1, source_target_pairs={{0,16},{2,18},{4,20},{6,22},{8,24},{10,26},{12,28},{14,30},{16,0},... | collective-permute-start | bytes 1572872 | tf_op jit(solution)/shard_map/ppermute | solution.py:13
  318.4 3.6 %copy-start.1 = (bf16[256,512]{1,0:T(8,128)(2,1)S(1)}, bf16[256,512]{1,0:T(8,128)(2,1)}, u32[]{:S(2)}) copy-start(bf16[256,512]{1,0:T(8,128)(2,1)} %param.15) | copy-start | bytes 786436
Sparse Core Ops, SparseCore 0:
  78.9 22.9 all-reduce.1
  111.9 44.1 reduce-scatter.1
  158.2 54.5 all-gather.3
  214.2 47.1 all-gather.5
